TPU v7x, 32 devices: a whole 2x2x4 slice. The times are simulated.
32 devices in a mesh: wide: 16 (over z, x, core), pair: 2 (over y).
Axes of the slice: x: 2, y: 2, z: 4, core: 2. Of those that a mesh axis runs over, the one named last changes fastest.
Arguments:
- pooled_b: bfloat16 [32, 16, 512, 128], P('wide', None, 'pair'), may hold values from -6 to 6
- dense_output_second: bfloat16 [8192, 128], P(('wide', 'pair')), may hold values from -4 to 4
- counts_b: int32 [8192, 26], P(('wide', 'pair')), may hold values from 1 to 8
- slot_of: int32 [32], replicated, may hold values from 0 to 31, each once
- stacked_a: bfloat16 [8192, 3456], P(('wide', 'pair')), may hold values from -4 to 4
- upstream_a: bfloat16 [8192, 3456], P(('wide', 'pair')), may hold values from -2 to 2
- counts_a: int32 [8192, 26], P(('wide', 'pair')), may hold values from 1 to 8
- down_projection: bfloat16 [3456, 512], P('wide'), may hold values from -0.109375 to 0.109375
- proj_up: bfloat16 [512, 3456], P(None, 'wide'), may hold values from -0.25 to 0.25
- cross_layer_bias: bfloat16 [3456], P('wide'), may hold values from -3 to 3
Outputs:
- crossed_b: bfloat16 [8192, 3456], P(('wide', 'pair'))
- dense_grad_a: bfloat16 [8192, 128], P(('wide', 'pair'))
- pooled_grad_a: bfloat16 [32, 16, 512, 128], P('wide', None, 'pair')
- grad_down: float32 [3456, 512], P('wide')
- grad_up: float32 [512, 3456], P(None, 'wide')
- grad_bias: float32 [3456], P('wide')
Inputs may be any that keep to these rules, and one draw needn't show every extreme that they name: slot_of holds every slot once; its first 26 entries are the slots of tables 0 to 25, the rest are unused. Slot s lies on index s // 2 of wide.
All inputs are finite; a program needn't handle non-finite values.
Results may differ from a plain program's by a relative error of at most 0.0075.
Values may be sent and summed in bfloat16 or wider, within the bound.
A program may use at most 128 MiB of HBM per device.

v0:
```python
import jax
import jax.numpy as jnp
from jax import lax
from jax.sharding import PartitionSpec as P


def table_means(slot_rows, lookup_count, table_slots):
    picked = jnp.take(slot_rows, table_slots, axis=0).astype(jnp.float32)
    scaled = picked / jnp.transpose(lookup_count).astype(jnp.float32)[:, :, None]
    return jnp.transpose(scaled, (1, 0, 2)).reshape(scaled.shape[1], -1).astype(jnp.bfloat16)


def cross_forward(stacked, down, up):
    low_rank = jnp.dot(stacked, down, preferred_element_type=jnp.float32).astype(jnp.bfloat16)
    projected = jnp.dot(low_rank, up, preferred_element_type=jnp.float32)
    return (low_rank, projected)


def crossed_output(stacked, projected, bias):
    stacked_wide = stacked.astype(jnp.float32)
    return (stacked_wide * (projected + bias.astype(jnp.float32)) + stacked_wide).astype(
        jnp.bfloat16
    )


def cross_backward(stacked, upstream, lookup_count, down, up, bias, feature_index):
    low_rank, projected = cross_forward(stacked, down, up)
    stacked_wide = stacked.astype(jnp.float32)
    upstream_wide = upstream.astype(jnp.float32)
    scale_grad = upstream_wide * stacked_wide
    grad_bias = jnp.sum(scale_grad, axis=0)
    proj_grad = scale_grad.astype(jnp.bfloat16)
    over_rows = (((0,), (0,)), ((), ()))
    over_cols = (((1,), (1,)), ((), ()))
    grad_up = lax.dot_general(low_rank, proj_grad, over_rows, preferred_element_type=jnp.float32)
    low_grad = lax.dot_general(proj_grad, up, over_cols, preferred_element_type=jnp.float32).astype(
        jnp.bfloat16
    )
    grad_down = lax.dot_general(stacked, low_grad, over_rows, preferred_element_type=jnp.float32)
    input_grad = upstream_wide * (projected + bias.astype(jnp.float32)) + upstream_wide
    input_grad = input_grad + lax.dot_general(
        low_grad, down, over_cols, preferred_element_type=jnp.float32
    )
    rows = stacked.shape[0]
    dense_gradient = input_grad[:, :feature_index].astype(jnp.bfloat16)
    table_gradient = (
        input_grad[:, feature_index:].reshape(rows, -1, feature_index)
        / lookup_count.astype(jnp.float32)[:, :, None]
    )
    table_gradient = jnp.transpose(table_gradient, (1, 0, 2)).astype(jnp.bfloat16)
    return (dense_gradient, table_gradient, grad_down, grad_up, grad_bias)


def local(
    pooled_b,
    dense_output_second,
    counts_b,
    slot_of,
    stacked_a,
    upstream_a,
    counts_a,
    down_projection,
    proj_up,
    cross_layer_bias,
):
    feature_index = dense_output_second.shape[1]
    tables = counts_b.shape[1]
    table_slots = slot_of[:tables]
    arrived = lax.all_to_all(pooled_b, "wide", split_axis=1, concat_axis=0, tiled=True)
    slot_count = arrived.shape[0]
    samples = arrived.shape[2]
    down, up, bias = (
        lax.all_gather(down_projection, "wide", axis=0, tiled=True),
        lax.all_gather(proj_up, "wide", axis=1, tiled=True),
        lax.all_gather(cross_layer_bias, "wide", axis=0, tiled=True),
    )
    slot_rows = arrived.reshape(slot_count, samples, feature_index)
    stacked_b = jnp.concatenate(
        [dense_output_second, table_means(slot_rows, counts_b, table_slots)], axis=1
    )
    low_rank, projected = cross_forward(stacked_b, down, up)
    crossed_b = crossed_output(stacked_b, projected, bias)
    dense_gradient, table_gradient, grad_down, grad_up, grad_bias = cross_backward(
        stacked_a, upstream_a, counts_a, down, up, bias, feature_index
    )
    slot_selector = (
        table_slots[None, :] == jnp.arange(slot_count, dtype=jnp.int32)[:, None]
    ).astype(jnp.bfloat16)
    slot_grad = jnp.einsum(
        "qv,vxk->qxk", slot_selector, table_gradient, preferred_element_type=jnp.float32
    ).astype(jnp.bfloat16)
    returned = lax.all_to_all(
        slot_grad.reshape(slot_count, 1, samples, feature_index),
        "wide",
        split_axis=0,
        concat_axis=1,
        tiled=True,
    )
    shares = (
        lax.psum_scatter(grad_down, "wide", scatter_dimension=0, tiled=True),
        lax.psum_scatter(grad_up, "wide", scatter_dimension=1, tiled=True),
        lax.psum_scatter(grad_bias, "wide", scatter_dimension=0, tiled=True),
    )
    summed = (
        lax.psum(shares[0].astype(jnp.bfloat16), "pair").astype(jnp.float32),
        lax.psum(shares[1].astype(jnp.bfloat16), "pair").astype(jnp.float32),
        lax.psum(shares[2].astype(jnp.bfloat16), "pair").astype(jnp.float32),
    )
    return (crossed_b, dense_gradient, returned, summed[0], summed[1], summed[2])


def solution(mesh):
    return jax.shard_map(
        local,
        mesh=mesh,
        in_specs=(
            P("wide", None, "pair", None),
            P(("wide", "pair"), None),
            P(("wide", "pair"), None),
            P(),
            P(("wide", "pair"), None),
            P(("wide", "pair"), None),
            P(("wide", "pair"), None),
            P("wide", None),
            P(None, "wide"),
            P("wide"),
        ),
        out_specs=(
            P(("wide", "pair"), None),
            P(("wide", "pair"), None),
            P("wide", None, "pair", None),
            P("wide", None),
            P(None, "wide"),
            P("wide"),
        ),
        check_vma=False,
    )
```

profile of v0, /device:TPU:0, one launch (start us, length us, event | category | flops | bytes accessed | tf_op | source)
XLA Modules:
  0.0 427.8 jit_solution(16351802026620585940)
XLA Ops:
  7.2 0.0 all-gather.5.cloned.1.call-start
  7.2 0.7 all-gather.5.cloned.1.call-update
  7.9 0.0 all-gather.3.cloned.1.call-start
  7.9 0.7 all-gather.3.cloned.1.call-update
  8.6 0.0 copy-start
  8.7 0.0 reduce-scatter.7.cloned.1.call-start
  8.7 51.4 %all-gather.5.cloned.1.call-done = bf16[512,3456]{0,1:T(8,128)(2,1)} async-done(((bf16[512,216]{0,1:T(8,128)(2,1)}), bf16[512,3456]{0,1:T(8,128)(2,1)}) %all-gather.5.cloned.1.call-update) | async-done | bytes 3538960 | tf_op jit(solution)/shard_map/all_gather | solution.py:74
  60.1 4.2 convolution_convert_fusion
  64.3 0.0 copy-start.4
  64.3 0.7 copy-done.4
  65.0 4.1 convolution_bitcast_fusion
  69.1 8.1 %copy.35 = f32[3456,512]{1,0:T(8,128)} copy(f32[3456,512]{0,1:T(8,128)} %convolution_bitcast_fusion) | data formatting | bytes 14155776
  77.2 0.0 reduce-scatter.7.cloned.1.call-update
  77.2 0.0 copy-start.1
  77.2 0.0 reduce-scatter.5.cloned.1.call-start
  77.3 30.9 %all-gather.3.cloned.1.call-done = bf16[3456,512]{1,0:T(8,128)(2,1)} async-done(((bf16[216,512]{1,0:T(8,128)(2,1)}), bf16[3456,512]{1,0:T(8,128)(2,1)}) %all-gather.3.cloned.1.call-update) | async-done | bytes 3538960 | tf_op jit(solution)/shard_map/all_gather | solution.py:73
  108.2 3.1 convolution_convert_fusion.1
  111.3 0.0 copy-start.6
  111.3 0.7 copy-done.6
  112.0 4.1 fusion.9
  116.1 0.0 reduce-scatter.5.cloned.1.call-update
  116.1 0.0 copy-start.8
  116.1 0.0 copy-start.10
  116.1 3.2 copy.27
  119.3 4.5 %all-to-all-start = ((bf16[2,16,256,128]{3,2,0,1:T(8,128)(2,1)}), bf16[2,16,256,128]{3,2,0,1:T(8,128)(2,1)}, u32[]{:S(2)}, u32[]{:S(2)}) async-start(bf16[2,16,256,128]{3,2,0,1:T(8,128)(2,1)} %copy.27), calls=%async_computation | async-start | bytes 4194304 | tf_op jit(solution)/shard_map/all_to_all | solution.py:69
  123.8 0.6 fusion.17
  125.0 0.2 dynamic-update-slice
  125.3 79.6 %all-reduce = bf16[3456]{0:T(1024)(128)(2,1)} all-reduce(bf16[3456]{0:T(1024)(128)(2,1)S(1)} %dynamic-update-slice), channel_id=1, replica_groups=mesh['wide'=16,'pair'=2] {'wide'}, use_global_device_ids=true, to_apply=%add | all-reduce | flops 3456 | bytes 13824
  204.9 0.7 convert_element_type.84
  205.6 1.4 convert_element_type.91
  206.9 3.4 fusion.1
  210.3 1.1 convolution_add_fusion
  211.5 1.7 copy-done.2
  213.3 2.1 slice.16
  215.3 5.0 %copy.30 = f32[256,3328]{0,1:T(8,128)} copy(f32[256,3328]{1,0:T(8,128)} %slice.16) | data formatting | bytes 6815744 | tf_op jit(solution)/shard_map/slice | solution.py:47
  220.4 3.6 fusion.8
  223.9 4.5 %copy.31 = bf16[26,256,128]{2,0,1:T(8,128)(2,1)} copy(bf16[26,256,128]{1,2,0:T(8,128)(2,1)} %fusion.8) | data formatting | bytes 3407872 | tf_op jit(solution)/shard_map/convert_element_type | solution.py:50
  228.4 2.3 convert_bitcast_fusion
  230.7 2.1 copy.32
  232.8 0.0 all-to-all-done
  232.8 22.1 %all-to-all-start.1 = ((bf16[32,1,256,128]{3,2,1,0:T(8,128)(2,1)}), bf16[32,1,256,128]{3,2,1,0:T(8,128)(2,1)}, u32[]{:S(2)}, u32[]{:S(2)}) async-start(bf16[32,1,256,128]{3,2,1,0:T(8,128)(2,1)} %copy.32), calls=%async_computation.1 | async-start | bytes 4194304 | tf_op jit(solution)/shard_map/all_to_all | solution.py:92
  254.9 0.0 all-reduce.5.cloned.1.call-start
  255.0 1.4 convert_element_type.79
  257.0 1.1 fusion.6
  258.1 115.6 %all-reduce.1 = bf16[3456]{0:T(1024)(128)(2,1)S(1)} all-reduce(f32[3456]{0:T(1024)} %fusion.6), channel_id=4, replica_groups=mesh['wide'=16,'pair'=2] {'wide'}, use_global_device_ids=true, to_apply=%region_5.6.clone | all-reduce | flops 3456 | bytes 20736
  373.8 0.1 dynamic-slice.4
  373.8 5.1 %psum.23 = bf16[216]{0:T(256)(128)(2,1)S(1)} all-reduce(bf16[216]{0:T(256)(128)(2,1)S(1)} %dynamic-slice.4), channel_id=1, replica_groups=mesh['wide'=16,'pair'=2] {'pair'}, use_global_device_ids=true, to_apply=%region_6.7 | all-reduce | flops 216 | bytes 864 | tf_op jit(solution)/shard_map/psum | solution.py:107
  378.9 0.6 convert_element_type.100
  379.5 0.7 compare_and_fusion
  380.2 2.5 gather_fusion
  382.6 1.2 fusion.5
  383.8 1.8 copy.28
  385.6 0.0 copy-start.9
  385.6 1.3 copy.29
  386.9 1.5 slice.19
  388.4 1.9 copy.36
  390.3 1.7 convert_element_type.97
  392.0 0.0 all-reduce.5.cloned.1.call-update
  392.1 6.6 %fusion.4 = bf16[256,3456]{1,0:T(8,128)(2,1)} fusion(bf16[512,3456]{0,1:T(8,128)(2,1)} %all-gather.5.cloned.1.call-done, f32[3456]{0:T(1024)S(1)} %convert_element_type.84, bf16[256,3328]{1,0:T(8,128)(2,1)S(1)} %copy.29, bf16[256,128]{1,0:T(8,128)(2,1)S(1)} %copy-done.9, bf16[3456,512]{1,0:T(8,128)(2,1)} %all-gather.3.cloned.1.call-done), kind=kOutput, calls=%fused_computation.9 | convolution fusion | flops 1822687232 | bytes 10630656 | tf_op jit(solution)/shard_map/dot_general | solution.py:15
  398.6 0.0 all-to-all-done.1
  398.6 3.1 copy.38
  401.8 15.9 %all-reduce.5.cloned.1.call-done = (bf16[216,512]{0,1:T(8,128)(2,1)}, bf16[512,216]{0,1:T(8,128)(2,1)}) async-done(((bf16[216,512]{0,1:T(8,128)(2,1)}, bf16[512,216]{0,1:T(8,128)(2,1)}), (bf16[216,512]{0,1:T(8,128)(2,1)}, bf16[512,216]{0,1:T(8,128)(2,1)})) %all-reduce.5.cloned.1.call-update) | async-done | bytes 442384 | tf_op jit(solution)/shard_map/psum | solution.py:105
  417.7 1.7 convert_element_type.98
  419.4 1.8 copy.34
  (16 shorter events, 0.0 us)
Async XLA Ops:
  7.2 53.0 %all-gather.5.cloned.1.call-start = ((), (), s32[]{:S(2)}) async-start(), calls=%async_computation.5 | async-start | bytes 3760128 | tf_op jit(solution)/shard_map/all_gather | solution.py:74
  7.9 100.3 %all-gather.3.cloned.1.call-start = ((), (), s32[]{:S(2)}) async-start(), calls=%async_computation.4 | async-start | bytes 3760128 | tf_op jit(solution)/shard_map/all_gather | solution.py:73
  8.6 56.4 %copy-start = (bf16[256,3456]{1,0:T(8,128)(2,1)S(1)}, bf16[256,3456]{1,0:T(8,128)(2,1)}, u32[]{:S(2)}) copy-start(bf16[256,3456]{1,0:T(8,128)(2,1)} %param.14) | copy-start | bytes 5308420
  8.7 379.8 %reduce-scatter.7.cloned.1.call-start = ((), (), s32[]{:S(2)}) async-start(), calls=%async_computation.7 | async-start | bytes 7520256
  64.3 0.7 copy-start.4
  77.2 34.8 %copy-start.1 = (bf16[256,3456]{1,0:T(8,128)(2,1)S(1)}, bf16[256,3456]{1,0:T(8,128)(2,1)}, u32[]{:S(2)}) copy-start(bf16[256,3456]{1,0:T(8,128)(2,1)} %param.15) | copy-start | bytes 5308420
  77.2 313.1 %reduce-scatter.5.cloned.1.call-start = ((), (), s32[]{:S(2)}) async-start(), calls=%async_computation.6 | async-start | bytes 7520256 | tf_op jit(solution)/shard_map/reduce_scatter | solution.py:101
  111.3 0.7 copy-start.6
  116.1 7.7 %copy-start.8 = (u32[32]{0:T(128)S(1)}, u32[32]{0:T(128)}, u32[]{:S(2)}) copy-start(u32[32]{0:T(128)} %constant.24) | copy-start | bytes 388
  116.1 8.9 %copy-start.10 = (bf16[216]{0:T(256)(128)(2,1)S(1)}, bf16[216]{0:T(256)(128)(2,1)}, u32[]{:S(2)}) copy-start(bf16[216]{0:T(256)(128)(2,1)} %param.19) | copy-start | bytes 1300
  119.3 113.5 %all-to-all-start = ((bf16[2,16,256,128]{3,2,0,1:T(8,128)(2,1)}), bf16[2,16,256,128]{3,2,0,1:T(8,128)(2,1)}, u32[]{:S(2)}, u32[]{:S(2)}) async-start(bf16[2,16,256,128]{3,2,0,1:T(8,128)(2,1)} %copy.27), calls=%async_computation | async-start | bytes 4194304 | tf_op jit(solution)/shard_map/all_to_all | solution.py:69
  206.9 3.4 copy-start.3
  206.9 3.4 copy-start.5
  211.5 1.7 copy-start.2
  232.8 165.8 %all-to-all-start.1 = ((bf16[32,1,256,128]{3,2,1,0:T(8,128)(2,1)}), bf16[32,1,256,128]{3,2,1,0:T(8,128)(2,1)}, u32[]{:S(2)}, u32[]{:S(2)}) async-start(bf16[32,1,256,128]{3,2,1,0:T(8,128)(2,1)} %copy.32), calls=%async_computation.1 | async-start | bytes 4194304 | tf_op jit(solution)/shard_map/all_to_all | solution.py:92
  254.9 162.7 %all-reduce.5.cloned.1.call-start = ((), (), s32[]{:S(2)}) async-start(), calls=%async_computation.8 | async-start | bytes 966656 | tf_op jit(solution)/shard_map/psum | solution.py:105
  258.1 124.5 %copy-start.7 = (f32[256,26]{0,1:T(8,128)S(1)}, f32[256,26]{0,1:T(8,128)}, u32[]{:S(2)}) copy-start(f32[256,26]{0,1:T(8,128)} %convert_element_type.79) | copy-start | bytes 79876
  385.6 6.5 %copy-start.9 = (bf16[256,128]{1,0:T(8,128)(2,1)S(1)}, bf16[256,128]{1,0:T(8,128)(2,1)}, u32[]{:S(2)}) copy-start(bf16[256,128]{1,0:T(8,128)(2,1)} %param.11) | copy-start | bytes 196612
Sparse Core Ops, SparseCore 0:
  10.3 49.8 all-gather.4
  62.4 45.7 all-gather.2
  112.2 111.3 reduce-scatter.6
  227.4 121.7 reduce-scatter.4
  392.2 25.4 all-reduce.4
where the time goes:
time: 429 us; the launch traced here: 428 us
  blocking collectives  200 us (47%)
  waiting for transfers between devices  99.7 us (23%)
  local copies, waits for them, and re-layouts  42.9 us (10%)
  matrix products  28.8 us (7%)
  starting transfers between devices  26.8 us (6%)
  between operations  15.3 us (4%)
  other arithmetic  14 us (3%)
    unnamed x2, blocking collectives  195 us
    all_gather x1, waiting for transfers between devices, local(): lax.all_gather(proj_up, 'wide', axis=1, tiled=True)  51.4 us
    all_gather x1, waiting for transfers between devices, local(): lax.all_gather(down_projection, 'wide', axis=0, tiled=True)  30.9 us
    all_to_all x1, starting transfers between devices, local(): lax.all_to_all(slot_grad.reshape(slot_count, 1, samples, feature_index),...  22.1 us
    unnamed x30, local copies, waits for them, and re-layouts  19 us
    psum x1, waiting for transfers between devices, local(): lax.psum(shares[0].astype(jnp.bfloat16), 'pair').astype(jnp.float32)  15.9 us
    dot_general x2, matrix products, cross_forward(): projected = jnp.dot(low_rank, up, preferred_element_type=jnp.float32)  9.97 us
  transfers between devices with their start and end apart: 7, of which 3 were waited for; matrix products, arithmetic and copies ran while one was open for 18% of the time, Pallas kernels for 0%

commit v1 on v0

--- a/solution.py
+++ b/solution.py
@@ -71,7 +71,7 @@
     samples = arrived.shape[2]
     down, up, bias = (
         lax.all_gather(down_projection, "wide", axis=0, tiled=True),
-        lax.all_gather(proj_up, "wide", axis=1, tiled=True),
+        jnp.concatenate(lax.all_gather(proj_up, "wide"), axis=1),
         lax.all_gather(cross_layer_bias, "wide", axis=0, tiled=True),
     )
     slot_rows = arrived.reshape(slot_count, samples, feature_index)

time: 429 us -> 433 us (level)
  local copies, waits for them, and re-layouts: 42.9 us -> 52.5 us
    unnamed x30 -> x33, local copies, waits for them, and re-layouts: 19 us -> 23.1 us
  transfers between devices with their start and end apart: 7 -> 7, of which waited for: 3 -> 3; matrix products, arithmetic and copies ran while one was open for 18% -> 20% of each run, Pallas kernels for 0% -> 0%
where the time goes in v1:
time: 433 us; the launch traced here: 432 us
  blocking collectives  200 us (46%)
  waiting for transfers between devices  98.2 us (23%)
  local copies, waits for them, and re-layouts  52.5 us (12%)
  starting transfers between devices  26.4 us (6%)
  matrix products  25.7 us (6%)
  between operations  15.3 us (4%)
  other arithmetic  14 us (3%)
    unnamed x2, blocking collectives  195 us
    all_gather x1, waiting for transfers between devices, local(): lax.all_gather(proj_up, 'wide')  53 us
    all_gather x1, waiting for transfers between devices, local(): lax.all_gather(down_projection, 'wide', axis=0, tiled=True)  27.5 us
    unnamed x33, local copies, waits for them, and re-layouts  23.1 us
    all_to_all x1, starting transfers between devices, local(): lax.all_to_all(slot_grad.reshape(slot_count, 1, samples, feature_index),...  21.7 us
    psum x1, waiting for transfers between devices, local(): lax.psum(shares[0].astype(jnp.bfloat16), 'pair').astype(jnp.float32)  16.3 us
    dot_general x2, matrix products, cross_forward(): projected = jnp.dot(low_rank, up, preferred_element_type=jnp.float32)  9.94 us
  transfers between devices with their start and end apart: 7, of which 3 were waited for; matrix products, arithmetic and copies ran while one was open for 20% of the time, Pallas kernels for 0%

profile of v1, /device:TPU:0, one launch (start us, length us, event | category | flops | bytes accessed | tf_op | source)
XLA Modules:
  0.0 432.3 jit_solution(3064193255996439607)
XLA Ops:
  7.2 0.0 all-gather.6.cloned.1.call-start
  7.2 0.7 all-gather.6.cloned.1.call-update
  7.9 0.0 all-gather.4.cloned.1.call-start
  7.9 0.7 all-gather.4.cloned.1.call-update
  8.6 0.0 reduce-scatter.7.cloned.1.call-start
  8.7 53.0 %all-gather.6.cloned.1.call-done = bf16[8192,216]{0,1:T(8,128)(2,1)} async-done(((bf16[512,216]{0,1:T(8,128)(2,1)}), bf16[8192,216]{0,1:T(8,128)(2,1)}) %all-gather.6.cloned.1.call-update) | async-done | bytes 3538960 | tf_op jit(solution)/shard_map/all_gather | solution.py:74
  61.7 3.5 copy.46
  65.2 0.0 copy-start
  65.3 0.0 copy-start.1
  65.3 2.0 copy.38
  67.3 1.1 convolution_convert_fusion
  68.5 0.6 copy-done.2
  69.0 0.7 copy-done.6
  69.7 4.1 convolution_bitcast_fusion
  73.8 8.0 %copy.44 = f32[3456,512]{1,0:T(8,128)} copy(f32[3456,512]{0,1:T(8,128)} %convolution_bitcast_fusion) | data formatting | bytes 14155776
  81.8 0.0 reduce-scatter.7.cloned.1.call-update
  81.8 0.0 reduce-scatter.5.cloned.1.call-start
  81.9 27.5 %all-gather.4.cloned.1.call-done = bf16[3456,512]{1,0:T(8,128)(2,1)} async-done(((bf16[216,512]{1,0:T(8,128)(2,1)}), bf16[3456,512]{1,0:T(8,128)(2,1)}) %all-gather.4.cloned.1.call-update) | async-done | bytes 3538960 | tf_op jit(solution)/shard_map/all_gather | solution.py:73
  109.3 3.1 convolution_convert_fusion.1
  112.5 0.0 copy-start.8
  112.5 0.7 copy-done.8
  113.2 4.1 fusion.9
  117.2 0.0 reduce-scatter.5.cloned.1.call-update
  117.3 0.0 copy-start.10
  117.3 0.0 copy-start.11
  117.3 3.2 copy.35
  120.4 4.5 %all-to-all-start = ((bf16[2,16,256,128]{3,2,0,1:T(8,128)(2,1)}), bf16[2,16,256,128]{3,2,0,1:T(8,128)(2,1)}, u32[]{:S(2)}, u32[]{:S(2)}) async-start(bf16[2,16,256,128]{3,2,0,1:T(8,128)(2,1)} %copy.35), calls=%async_computation | async-start | bytes 4194304 | tf_op jit(solution)/shard_map/all_to_all | solution.py:69
  124.9 0.6 fusion.17
  126.2 0.2 dynamic-update-slice
  126.4 79.6 %all-reduce = bf16[3456]{0:T(1024)(128)(2,1)} all-reduce(bf16[3456]{0:T(1024)(128)(2,1)S(1)} %dynamic-update-slice), channel_id=1, replica_groups=mesh['wide'=16,'pair'=2] {'wide'}, use_global_device_ids=true, to_apply=%add | all-reduce | flops 3456 | bytes 13824
  206.0 0.7 convert_element_type.84
  206.7 1.4 convert_element_type.91
  208.1 3.4 fusion.1
  211.5 1.1 convolution_add_fusion
  212.7 1.8 copy-done.4
  214.4 2.1 slice.16
  216.5 5.0 %copy.39 = f32[256,3328]{0,1:T(8,128)} copy(f32[256,3328]{1,0:T(8,128)} %slice.16) | data formatting | bytes 6815744 | tf_op jit(solution)/shard_map/slice | solution.py:47
  221.5 3.6 fusion.8
  225.1 4.5 %copy.40 = bf16[26,256,128]{2,0,1:T(8,128)(2,1)} copy(bf16[26,256,128]{1,2,0:T(8,128)(2,1)} %fusion.8) | data formatting | bytes 3407872 | tf_op jit(solution)/shard_map/convert_element_type | solution.py:50
  229.6 2.3 convert_bitcast_fusion
  231.9 2.1 copy.41
  234.0 0.0 all-to-all-done
  234.0 21.7 %all-to-all-start.1 = ((bf16[32,1,256,128]{3,2,1,0:T(8,128)(2,1)}), bf16[32,1,256,128]{3,2,1,0:T(8,128)(2,1)}, u32[]{:S(2)}, u32[]{:S(2)}) async-start(bf16[32,1,256,128]{3,2,1,0:T(8,128)(2,1)} %copy.41), calls=%async_computation.1 | async-start | bytes 4194304 | tf_op jit(solution)/shard_map/all_to_all | solution.py:92
  255.7 0.0 all-reduce.5.cloned.1.call-start
  255.8 1.4 convert_element_type.79
  257.8 1.1 fusion.6
  258.9 115.1 %all-reduce.1 = bf16[3456]{0:T(1024)(128)(2,1)S(1)} all-reduce(f32[3456]{0:T(1024)} %fusion.6), channel_id=5, replica_groups=mesh['wide'=16,'pair'=2] {'wide'}, use_global_device_ids=true, to_apply=%region_5.6.clone | all-reduce | flops 3456 | bytes 20736
  374.0 0.1 dynamic-slice.4
  374.1 5.5 %psum.23 = bf16[216]{0:T(256)(128)(2,1)S(1)} all-reduce(bf16[216]{0:T(256)(128)(2,1)S(1)} %dynamic-slice.4), channel_id=1, replica_groups=mesh['wide'=16,'pair'=2] {'pair'}, use_global_device_ids=true, to_apply=%region_6.7 | all-reduce | flops 216 | bytes 864 | tf_op jit(solution)/shard_map/psum | solution.py:107
  379.5 0.6 convert_element_type.100
  380.1 0.7 compare_and_fusion
  380.8 2.5 gather_fusion
  383.2 1.2 fusion.5
  384.4 2.7 copy.36
  387.1 3.9 copy.37
  391.0 1.5 slice.19
  392.6 1.9 copy.45
  394.4 1.7 convert_element_type.97
  396.1 0.0 all-reduce.5.cloned.1.call-update
  396.2 6.6 %fusion.4 = bf16[256,3456]{1,0:T(8,128)(2,1)} fusion(bf16[512,3456]{0,1:T(8,128)(2,1)S(1)} %bitcast.52, f32[3456]{0:T(1024)S(1)} %convert_element_type.84, bf16[256,3328]{1,0:T(8,128)(2,1)} %copy.37, bf16[256,128]{1,0:T(8,128)(2,1)} %param.11, bf16[3456,512]{1,0:T(8,128)(2,1)} %all-gather.4.cloned.1.call-done), kind=kOutput, calls=%fused_computation.9 | convolution fusion | flops 1822687232 | bytes 10630656 | tf_op jit(solution)/shard_map/dot_general | solution.py:15
  402.7 3.1 copy.48
  405.9 16.3 %all-reduce.5.cloned.1.call-done = (bf16[216,512]{0,1:T(8,128)(2,1)}, bf16[512,216]{0,1:T(8,128)(2,1)}) async-done(((bf16[216,512]{0,1:T(8,128)(2,1)}, bf16[512,216]{0,1:T(8,128)(2,1)}), (bf16[216,512]{0,1:T(8,128)(2,1)}, bf16[512,216]{0,1:T(8,128)(2,1)})) %all-reduce.5.cloned.1.call-update) | async-done | bytes 442384 | tf_op jit(solution)/shard_map/psum | solution.py:105
  422.1 1.7 convert_element_type.98
  423.9 1.8 copy.43
  (20 shorter events, 0.0 us)
Async XLA Ops:
  7.2 54.6 %all-gather.6.cloned.1.call-start = ((), (), s32[]{:S(2)}) async-start(), calls=%async_computation.6 | async-start | bytes 3760128 | tf_op jit(solution)/shard_map/all_gather | solution.py:74
  7.9 101.4 %all-gather.4.cloned.1.call-start = ((), (), s32[]{:S(2)}) async-start(), calls=%async_computation.4 | async-start | bytes 3760128 | tf_op jit(solution)/shard_map/all_gather | solution.py:73
  8.6 383.9 %reduce-scatter.7.cloned.1.call-start = ((), (), s32[]{:S(2)}) async-start(), calls=%async_computation.7 | async-start | bytes 7520256
  65.2 2.0 copy-start
  65.3 2.0 copy-start.1
  67.3 1.7 copy-start.2
  69.0 0.7 copy-start.6
  81.8 312.6 %reduce-scatter.5.cloned.1.call-start = ((), (), s32[]{:S(2)}) async-start(), calls=%async_computation.5 | async-start | bytes 7520256 | tf_op jit(solution)/shard_map/reduce_scatter | solution.py:101
  112.5 0.7 copy-start.8
  117.3 7.6 %copy-start.10 = (u32[32]{0:T(128)S(1)}, u32[32]{0:T(128)}, u32[]{:S(2)}) copy-start(u32[32]{0:T(128)} %constant.24) | copy-start | bytes 388
  117.3 8.9 %copy-start.11 = (bf16[216]{0:T(256)(128)(2,1)S(1)}, bf16[216]{0:T(256)(128)(2,1)}, u32[]{:S(2)}) copy-start(bf16[216]{0:T(256)(128)(2,1)} %param.19) | copy-start | bytes 1300
  120.4 113.6 %all-to-all-start = ((bf16[2,16,256,128]{3,2,0,1:T(8,128)(2,1)}), bf16[2,16,256,128]{3,2,0,1:T(8,128)(2,1)}, u32[]{:S(2)}, u32[]{:S(2)}) async-start(bf16[2,16,256,128]{3,2,0,1:T(8,128)(2,1)} %copy.35), calls=%async_computation | async-start | bytes 4194304 | tf_op jit(solution)/shard_map/all_to_all | solution.py:69
  208.1 3.4 copy-start.5
  208.1 3.4 copy-start.7
  212.7 1.8 copy-start.4
  234.0 168.7 %all-to-all-start.1 = ((bf16[32,1,256,128]{3,2,1,0:T(8,128)(2,1)}), bf16[32,1,256,128]{3,2,1,0:T(8,128)(2,1)}, u32[]{:S(2)}, u32[]{:S(2)}) async-start(bf16[32,1,256,128]{3,2,1,0:T(8,128)(2,1)} %copy.41), calls=%async_computation.1 | async-start | bytes 4194304 | tf_op jit(solution)/shard_map/all_to_all | solution.py:92
  255.7 166.4 %all-reduce.5.cloned.1.call-start = ((), (), s32[]{:S(2)}) async-start(), calls=%async_computation.8 | async-start | bytes 966656 | tf_op jit(solution)/shard_map/psum | solution.py:105
  258.9 124.3 %copy-start.9 = (f32[256,26]{0,1:T(8,128)S(1)}, f32[256,26]{0,1:T(8,128)}, u32[]{:S(2)}) copy-start(f32[256,26]{0,1:T(8,128)} %convert_element_type.79) | copy-start | bytes 79876
  387.1 9.1 %copy-start.3 = (bf16[512,16,216]{0,2,1:T(8,128)(2,1)S(1)}, bf16[512,16,216]{0,2,1:T(8,128)(2,1)}, u32[]{:S(2)}) copy-start(bf16[512,16,216]{0,2,1:T(8,128)(2,1)} %copy-done.2) | copy-start | bytes 10616836
Sparse Core Ops, SparseCore 0:
  10.1 51.5 all-gather.5
  64.0 45.2 all-gather.3
  113.4 111.3 reduce-scatter.6
  228.6 121.7 reduce-scatter.4
  396.3 25.8 all-reduce.4
